TPU v7x, 32 devices: a whole 2x2x4 slice. The times are simulated.
32 devices in a mesh: tm: 4 (over y, x), sky: 8 (over z, core).
Axes of the slice: x: 2, y: 2, z: 4, core: 2. Of those that a mesh axis runs over, the one named last changes fastest.
Arguments:
- residual: float32 [16384, 128], P(('tm', 'sky')), may hold values from -110 to 110
- obs_weight: float32 [16384, 128], P(('tm', 'sky')), may hold values from 0.5 to 2
- source_partials: float32 [5, 16384, 128], P(None, ('tm', 'sky')), may hold values from -1 to 1
- attitude_partials: float32 [16, 16384, 128], P(None, ('tm', 'sky')), may hold values from -1.5 to 1.5
- source_index: int32 [16384, 128], P(('tm', 'sky')), may hold values from 0 to 127
- tile_pixel: int32 [16384], P(('tm', 'sky')), may hold values from 0 to 1023, as said below
- tile_knot: int32 [16384], P(('tm', 'sky')), may hold values from 0 to 2047, as said below
- pixel_slot: int32 [1024], replicated, may hold values from 0 to 1023, as said below
Outputs:
- final_residual: float32 [16384, 128], P(('tm', 'sky'))
- source_update: float32 [5, 131072], P(None, 'sky')
- attitude_update: float32 [4, 2048], P(None, 'tm')
Inputs may be any that keep to these rules, and one draw needn't show every extreme that they name: Tiles come in aligned blocks of 512; with owner = pixel_slot[tile_pixel[t]] // 128, no block holds more than 192 tiles of one owner, and every block holds exactly 192 tiles of some owner. `pixel_slot`: every slot number appears once. `tile_knot`: the tiles of aligned block q of 512 tiles have first knots in [q * 64, (q + 1) * 64).
All inputs are finite; a program needn't handle non-finite values.
Results may differ from a plain program's by a relative error of at most 0.0003.
Values sent between devices are 32-bit elements; how exact they have to be, the bound alone decides.
A program may use at most 128 MiB of HBM per device.

v0:
```python
import math

import jax
import jax.numpy as jnp
from jax import lax
from jax.sharding import PartitionSpec as P

PIX_DEV = 128
SRC_PIX = 128
KNOTS_DEV = 512


SOURCE_PAIRS = tuple(((first, second) for first in range(5) for second in range(first, 5)))
KNOT_PAIRS = tuple(((first, second) for first in range(4) for second in range(first, 4)))


def passed_along(value, axis, steps):
    count = lax.axis_size(axis)
    first, last = (max(0, -steps), min(count, count - steps))
    return lax.ppermute(value, axis, [(source, source + steps) for source in range(first, last)])


def damped_solve(normal, target, order, pairs):
    entries = {}
    for number, couple in enumerate(pairs):
        entries[couple] = normal[number]
    factor = {}
    for column in range(order):
        pivot_value = entries[column, column] + 1.0
        for earlier in range(column):
            pivot_value = pivot_value - factor[column, earlier] * factor[column, earlier]
        pivot_value = jnp.sqrt(pivot_value)
        factor[column, column] = pivot_value
        for below in range(column + 1, order):
            current = entries[column, below]
            for earlier in range(column):
                current = current - factor[below, earlier] * factor[column, earlier]
            factor[below, column] = current / pivot_value
    forward = []
    for column in range(order):
        current = target[column]
        for earlier in range(column):
            current = current - factor[column, earlier] * forward[earlier]
        forward.append(current / factor[column, column])
    answer = [None] * order
    for column in reversed(range(order)):
        current = forward[column]
        for later in range(column + 1, order):
            current = current - factor[later, column] * answer[later]
        answer[column] = current / factor[column, column]
    return jnp.stack(answer)


def knot_terms(weights, partials, baseline):
    result = []
    for segment in range(4):
        portion = partials[4 * segment : 4 * segment + 4]
        sums_rows = [
            jnp.sum(weights * portion[first] * portion[second], axis=-1)
            for first, second in KNOT_PAIRS
        ]
        sums_rows = sums_rows + [
            jnp.sum(weights * portion[first] * baseline, axis=-1) for first in range(4)
        ]
        result.append(jnp.stack(sums_rows))
    return result


def correct(baseline, partials, picked):
    accumulated = partials[0] * picked[0]
    for component in range(1, partials.shape[0]):
        accumulated = accumulated + partials[component] * picked[component]
    return baseline - accumulated


def pixel_sums(products, indices, owners, capacity):

    def add_sender(sender, running):
        offset = sender * capacity
        portion = lax.dynamic_slice_in_dim(products, offset, capacity, 1)
        chosen = lax.dynamic_slice_in_dim(indices, offset, capacity, 0)
        within = ((chosen % SRC_PIX)[:, :, None] == jnp.arange(SRC_PIX, dtype=jnp.int32)).astype(
            jnp.float32
        )
        pixel_hits = (
            (chosen[:, 0] // SRC_PIX)[:, None] == jnp.arange(PIX_DEV, dtype=jnp.int32)
        ).astype(jnp.float32)
        spread = jnp.einsum("ctk,tks->cts", portion, within, precision=lax.Precision.HIGHEST)
        return running + jnp.einsum(
            "cts,tp->cps", spread, pixel_hits, precision=lax.Precision.HIGHEST
        )

    running = lax.fori_loop(0, owners, add_sender, jnp.zeros((20, PIX_DEV, SRC_PIX), jnp.float32))
    return running.reshape(20, PIX_DEV * SRC_PIX)


def pick_sources(update, indices, rows):
    pixels = update.shape[1] // SRC_PIX
    table = update.reshape(update.shape[0], pixels, SRC_PIX)
    blocks = indices.shape[0] // rows

    def fill(number, output):
        offset = number * rows
        chosen = lax.dynamic_slice_in_dim(indices, offset, rows, 0)
        pixel_hits = (
            (chosen[:, 0] // SRC_PIX)[:, None] == jnp.arange(pixels, dtype=jnp.int32)
        ).astype(jnp.float32)
        within = ((chosen % SRC_PIX)[:, :, None] == jnp.arange(SRC_PIX, dtype=jnp.int32)).astype(
            jnp.float32
        )
        row_values = jnp.einsum("tp,cps->cts", pixel_hits, table, precision=lax.Precision.HIGHEST)
        picked = jnp.einsum("cts,tks->ctk", row_values, within, precision=lax.Precision.HIGHEST)
        return lax.dynamic_update_slice_in_dim(output, picked, offset, 1)

    empty = jnp.zeros((update.shape[0], indices.shape[0], indices.shape[1]), jnp.float32)
    return lax.fori_loop(0, blocks, fill, empty)


def body(
    residual,
    obs_weight,
    source_partials,
    attitude_partials,
    source_index,
    tile_pixel,
    tile_knot,
    pixel_slot,
):
    owners = lax.axis_size("sky")
    tiles = residual.shape[0]
    capacity = 3 * tiles // owners
    pixels = pixel_slot.shape[0]
    pixel_match = (tile_pixel[:, None] == jnp.arange(pixels, dtype=jnp.int32)[None, :]).astype(
        jnp.float32
    )
    seats_float = jnp.dot(
        pixel_match, pixel_slot.astype(jnp.float32), precision=lax.Precision.HIGHEST
    )
    seats = seats_float.astype(jnp.int32)
    owner_ids = seats // PIX_DEV
    local_pixel = seats % PIX_DEV
    member = (owner_ids[:, None] == jnp.arange(owners, dtype=jnp.int32)[None, :]).astype(
        jnp.float32
    )
    tile_numbers = jnp.arange(tiles, dtype=jnp.int32)
    lower = (tile_numbers[:, None] > tile_numbers[None, :]).astype(jnp.float32)
    before = jnp.dot(lower, member, precision=lax.Precision.HIGHEST)
    position = jnp.sum(before * member, axis=1).astype(jnp.int32)
    slot_index = owner_ids * capacity + position
    place = (jnp.arange(owners * capacity, dtype=jnp.int32)[:, None] == slot_index[None, :]).astype(
        jnp.float32
    )
    local_source = (local_pixel[:, None] * SRC_PIX + source_index).astype(jnp.float32)
    sent_index = jnp.dot(place, local_source, precision=lax.Precision.HIGHEST).astype(jnp.int32)[
        None
    ]
    root_weight = jnp.sqrt(obs_weight)
    fields = jnp.concatenate(
        [(root_weight * residual)[None], root_weight[None] * source_partials], axis=0
    )
    packed = jnp.einsum("st,ctk->csk", place, fields, precision=lax.Precision.HIGHEST)
    arrived, arrived_index = (
        lax.all_to_all(packed, "sky", split_axis=1, concat_axis=1, tiled=True),
        lax.all_to_all(sent_index, "sky", split_axis=1, concat_axis=1, tiled=True),
    )
    scaled = arrived[1:]
    products = [scaled[first] * scaled[second] for first, second in SOURCE_PAIRS]
    products = jnp.stack(products + [scaled[first] * arrived[0] for first in range(5)])
    normals = pixel_sums(products, arrived_index[0], owners, capacity)
    summed = lax.psum(normals, "tm")
    source_update = damped_solve(summed[:15], summed[15:], 5, SOURCE_PAIRS)
    everything = lax.all_gather(source_update, "sky", axis=1, tiled=True)
    global_source = seats[:, None] * SRC_PIX + source_index
    picked = pick_sources(everything, global_source, math.gcd(tiles, 64))
    settled = correct(residual, source_partials, picked)
    knot_start = tile_knot - lax.axis_index("tm") * KNOTS_DEV
    knot_hits = (knot_start[:, None] == jnp.arange(KNOTS_DEV, dtype=jnp.int32)[None, :]).astype(
        jnp.float32
    )
    accumulated = jnp.zeros((14, KNOTS_DEV + 3), jnp.float32)
    for segment, tile_sums in enumerate(knot_terms(obs_weight, attitude_partials, settled)):
        placed = jnp.dot(tile_sums, knot_hits, precision=lax.Precision.HIGHEST)
        accumulated = accumulated + jnp.pad(placed, ((0, 0), (segment, 3 - segment)))
    arriving = passed_along(accumulated[:, KNOTS_DEV:], "tm", 1)
    own_rows = accumulated[:, :KNOTS_DEV] + jnp.pad(arriving, ((0, 0), (0, KNOTS_DEV - 3)))
    whole = lax.psum(own_rows, "sky")
    attitude_update = damped_solve(whole[:10], whole[10:], 4, KNOT_PAIRS)
    following = passed_along(attitude_update[:, :3], "tm", -1)
    extended = jnp.concatenate([attitude_update, following], axis=1)
    accumulated_fix = None
    for segment in range(4):
        window = extended[:, segment : segment + KNOTS_DEV]
        values = jnp.dot(window, knot_hits.T, precision=lax.Precision.HIGHEST)
        for component in range(4):
            addend = attitude_partials[4 * segment + component] * values[component][:, None]
            accumulated_fix = addend if accumulated_fix is None else accumulated_fix + addend
    final_residual = settled - accumulated_fix
    return (final_residual, source_update, attitude_update)


def solution(mesh):
    in_specs = (
        P(("tm", "sky"), None),
        P(("tm", "sky"), None),
        P(None, ("tm", "sky"), None),
        P(None, ("tm", "sky"), None),
        P(("tm", "sky"), None),
        P(("tm", "sky")),
        P(("tm", "sky")),
        P(),
    )
    out_specs = (P(("tm", "sky"), None), P(None, "sky"), P(None, "tm"))
    return jax.shard_map(body, mesh=mesh, in_specs=in_specs, out_specs=out_specs, check_vma=False)
```

profile of v0, /device:TPU:5, one launch (start us, length us, event | category | flops | bytes accessed | tf_op | source)
XLA Modules:
  0.0 621.8 jit_solution(8565217620249601764)
XLA Ops:
  12.9 6.0 convolution_bitcast_fusion.1
  18.8 6.2 copy.44
  25.0 5.7 all-to-all-start.1
  33.2 135.5 %all-to-all-done.1 = f32[6,1536,128]{2,0,1:T(8,128)} async-done(((f32[6,1536,128]{2,0,1:T(8,128)}), f32[6,1536,128]{2,0,1:T(8,128)}, u32[]{:S(2)}, u32[]{:S(2)}) %all-to-all-start.1) | async-done | bytes 4718624 | tf_op jit(solution)/shard_map/all_to_all | solution.py:163
  168.8 5.1 all-to-all-start
  173.8 22.1 %slice_multiply_fusion = (f32[1,1536,128]{2,0,1:T(1,128)S(1)}, f32[1,1536,128]{2,0,1:T(1,128)S(1)}, f32[1,1536,128]{2,0,1:T(1,128)}, f32[1,1536,128]{2,0,1:T(1,1...) fusion(f32[6,1536,128]{2,0,1:T(8,128)} %all-to-all-done.1), kind=kLoop, calls=%fused_computation.340 | loop fusion | flops 2359296 | bytes 14155776 | tf_op jit(solution)/shard_map/mul | solution.py:168
  195.9 20.9 %slice_multiply_fusion.1 = (f32[1,1536,128]{2,0,1:T(1,128)}, f32[1,1536,128]{2,0,1:T(1,128)}, f32[1,1536,128]{2,0,1:T(1,128)}, f32[1,1536,128]{2,0,1:T(1,128)}, ...) fusion(f32[6,1536,128]{2,0,1:T(8,128)} %all-to-all-done.1), kind=kLoop, calls=%fused_computation.341 | loop fusion | flops 1572864 | bytes 11010048 | tf_op jit(solution)/shard_map/mul | solution.py:168
  216.9 49.6 %stack.218 = f32[20,1536,128]{2,0,1:T(8,128)} concatenate(f32[1,1536,128]{2,0,1:T(1,128)} %get-tuple-element.400, f32[1,1536,128]{2,0,1:T(1,128)} %get-tuple-element.408, f32[1,1536,128]{2,0,1:T(1,128)} %get-tuple-element.407, f32[1,1536,128]{2,0,1:T(1,128)} %get-tuple-element.406, f32[1,1536,128]{2,0,1:T(1,128)} %get-tuple-element.405, f32[1,1536,128]{2,0,1:T(1,128)S(1)} %get-tuple-element.390, ...), dimensions={0} | concatenate | bytes 31457280 | tf_op jit(solution)/shard_map/stack | solution.py:168
  266.5 114.9 %while.32 = (s32[]{:T(128)}, f32[20,128,128]{2,1,0:T(8,128)S(1)}, s32[1536,128]{1,0:T(8,128)}, f32[20,1536,128]{2,0,1:T(8,128)}, s32[]{:T(128)}, /*index=5*/s32[]{:T(128)}, s32[]{:T(128)}, s32[]{:T(128)}) while((s32[]{:T(128)}, f32[20,128,128]{2,1,0:T(8,128)S(1)}, s32[1536,128]{1,0:T(8,128)}, f32[20,1536,128]{2,0,1:T(8,128)}, ...), condition=%wide.region_2.3_spmd.clone, body=%wide.region_1.2_spmd.clone.sunk | while | flops 1514048256 | bytes 9800085 | solution.py:93
  267.7 9.9 %fusion.206 = f32[20,192,128]{2,0,1:T(8,128)} fusion(f32[20,1536,128]{2,0,1:T(8,128)} %get-tuple-element.501, s32[]{:T(128)S(6)} %select_n.124, s32[192,128]{1,0:T(8,128)S(1)} %copy.140), kind=kOutput, calls=%fused_computation.26.clone.1 | convolution fusion | flops 758120448 | bytes 4423684 | tf_op jit(solution)/shard_map/while/body/eval_jaxpr/ctk,tks->cts/dot_general | solution.py:88
  282.0 9.9 %fusion.206 = f32[20,192,128]{2,0,1:T(8,128)} fusion(f32[20,1536,128]{2,0,1:T(8,128)} %get-tuple-element.501, s32[]{:T(128)S(6)} %select_n.124, s32[192,128]{1,0:T(8,128)S(1)} %copy.140), kind=kOutput, calls=%fused_computation.26.clone.1 | convolution fusion | flops 758120448 | bytes 4423684 | tf_op jit(solution)/shard_map/while/body/eval_jaxpr/ctk,tks->cts/dot_general | solution.py:88
  296.4 9.9 %fusion.206 = f32[20,192,128]{2,0,1:T(8,128)} fusion(f32[20,1536,128]{2,0,1:T(8,128)} %get-tuple-element.501, s32[]{:T(128)S(6)} %select_n.124, s32[192,128]{1,0:T(8,128)S(1)} %copy.140), kind=kOutput, calls=%fused_computation.26.clone.1 | convolution fusion | flops 758120448 | bytes 4423684 | tf_op jit(solution)/shard_map/while/body/eval_jaxpr/ctk,tks->cts/dot_general | solution.py:88
  310.8 9.9 %fusion.206 = f32[20,192,128]{2,0,1:T(8,128)} fusion(f32[20,1536,128]{2,0,1:T(8,128)} %get-tuple-element.501, s32[]{:T(128)S(6)} %select_n.124, s32[192,128]{1,0:T(8,128)S(1)} %copy.140), kind=kOutput, calls=%fused_computation.26.clone.1 | convolution fusion | flops 758120448 | bytes 4423684 | tf_op jit(solution)/shard_map/while/body/eval_jaxpr/ctk,tks->cts/dot_general | solution.py:88
  325.1 9.9 %fusion.206 = f32[20,192,128]{2,0,1:T(8,128)} fusion(f32[20,1536,128]{2,0,1:T(8,128)} %get-tuple-element.501, s32[]{:T(128)S(6)} %select_n.124, s32[192,128]{1,0:T(8,128)S(1)} %copy.140), kind=kOutput, calls=%fused_computation.26.clone.1 | convolution fusion | flops 758120448 | bytes 4423684 | tf_op jit(solution)/shard_map/while/body/eval_jaxpr/ctk,tks->cts/dot_general | solution.py:88
  339.5 9.9 %fusion.206 = f32[20,192,128]{2,0,1:T(8,128)} fusion(f32[20,1536,128]{2,0,1:T(8,128)} %get-tuple-element.501, s32[]{:T(128)S(6)} %select_n.124, s32[192,128]{1,0:T(8,128)S(1)} %copy.140), kind=kOutput, calls=%fused_computation.26.clone.1 | convolution fusion | flops 758120448 | bytes 4423684 | tf_op jit(solution)/shard_map/while/body/eval_jaxpr/ctk,tks->cts/dot_general | solution.py:88
  353.8 9.9 %fusion.206 = f32[20,192,128]{2,0,1:T(8,128)} fusion(f32[20,1536,128]{2,0,1:T(8,128)} %get-tuple-element.501, s32[]{:T(128)S(6)} %select_n.124, s32[192,128]{1,0:T(8,128)S(1)} %copy.140), kind=kOutput, calls=%fused_computation.26.clone.1 | convolution fusion | flops 758120448 | bytes 4423684 | tf_op jit(solution)/shard_map/while/body/eval_jaxpr/ctk,tks->cts/dot_general | solution.py:88
  368.2 9.9 %fusion.206 = f32[20,192,128]{2,0,1:T(8,128)} fusion(f32[20,1536,128]{2,0,1:T(8,128)} %get-tuple-element.501, s32[]{:T(128)S(6)} %select_n.124, s32[192,128]{1,0:T(8,128)S(1)} %copy.140), kind=kOutput, calls=%fused_computation.26.clone.1 | convolution fusion | flops 758120448 | bytes 4423684 | tf_op jit(solution)/shard_map/while/body/eval_jaxpr/ctk,tks->cts/dot_general | solution.py:88
  383.9 61.1 %all-reduce.7.cloned.1.call-done = f32[20,16384]{1,0:T(8,128)} async-done(((f32[20,16384]{1,0:T(8,128)}), f32[20,16384]{1,0:T(8,128)}) %all-reduce.7.cloned.1.call-update) | async-done | bytes 1310736 | tf_op jit(solution)/shard_map/psum | solution.py:170
  445.0 5.2 fusion.141
  466.3 40.7 %all-gather.2.cloned.1.call-done = f32[5,131072]{1,0:T(8,128)} async-done(((f32[5,16384]{1,0:T(8,128)}), f32[5,131072]{1,0:T(8,128)}) %all-gather.2.cloned.1.call-update) | async-done | bytes 2621456 | tf_op jit(solution)/shard_map/all_gather | solution.py:172
  510.8 55.2 %while.31 = (s32[]{:T(128)}, f32[5,512,128]{2,1,0:T(8,128)}, s32[512,128]{0,1:T(8,128)S(1)}, f32[5,1024,128]{2,1,0:T(8,128)S(1)}, s32[]{:T(128)}, /*index=5*/s32[]{:T(128)}, s32[]{:T(128)}, s32[]{:T(128)}) while((s32[]{:T(128)}, f32[5,512,128]{2,1,0:T(8,128)}, s32[512,128]{0,1:T(8,128)S(1)}, f32[5,1024,128]{2,1,0:T(8,128)S(1)}, s32[]{:T(128)}, ...), condition=%wide.region_5.6_spmd, body=%wide.region_4.5_spmd.sunk | while | flops 567436224 | bytes 3605391 | solution.py:116
  512.2 4.8 fusion.202
  519.1 4.8 fusion.202
  579.9 23.3 %psum.15 = f32[14,512]{1,0:T(8,128)S(1)} all-reduce(f32[14,512]{1,0:T(8,128)S(1)} %slice_add_fusion.5), channel_id=1, replica_groups=mesh['tm'=4,'sky'=8] {'sky'}, use_global_device_ids=true, to_apply=%region_62.63 | all-reduce | flops 7168 | bytes 57344 | tf_op jit(solution)/shard_map/psum | solution.py:186
  (177 shorter events, 136.5 us)
Async XLA Ops:
  7.2 5.1 copy-start.1
  25.0 5.7 copy-start.8
  25.0 143.7 %all-to-all-start.1 = ((f32[6,1536,128]{2,0,1:T(8,128)}), f32[6,1536,128]{2,0,1:T(8,128)}, u32[]{:S(2)}, u32[]{:S(2)}) async-start(f32[6,1536,128]{2,0,1:T(8,128)} %copy.44), calls=%async_computation.1 | async-start | bytes 12582912 | tf_op jit(solution)/shard_map/all_to_all | solution.py:163
  168.8 97.7 %all-to-all-start = ((s32[1,1536,128]{2,0,1:T(1,128)}), s32[1,1536,128]{2,0,1:T(1,128)}, u32[]{:S(2)}, u32[]{:S(2)}) async-start(s32[1,1536,128]{2,0,1:T(1,128)} %bitcast.7), calls=%async_computation | async-start | bytes 1572864 | tf_op jit(solution)/shard_map/all_to_all | solution.py:164
  173.8 271.2 %all-reduce.7.cloned.1.call-start = ((), (), s32[]{:S(2)}) async-start(), calls=%async_computation.2 | async-start | bytes 3145728 | tf_op jit(solution)/shard_map/psum | solution.py:170
  383.6 123.3 %all-gather.2.cloned.1.call-start = ((), (), s32[]{:S(2)}) async-start(), calls=%async_computation.3 | async-start | bytes 4718592 | tf_op jit(solution)/shard_map/all_gather | solution.py:172
  454.2 5.2 copy-start.10
  454.2 5.3 copy-start.2
  566.0 3.7 copy-start
  566.0 3.7 copy-start.3
  566.0 3.8 copy-start.4
  566.0 3.9 copy-start.5
  566.0 3.9 copy-start.6
  566.0 4.0 copy-start.7
  574.6 5.3 collective-permute-start
  603.4 11.6 %copy-start.9 = (f32[4,512]{1,0:T(4,128)}, f32[4,512]{1,0:T(4,128)S(1)}, u32[]{:S(2)}) copy-start(f32[4,512]{1,0:T(4,128)S(1)} %pad_maximum_fusion.1) | copy-start | bytes 24580
  604.0 4.3 collective-permute-start.1
Sparse Core Ops, SparseCore 0:
  383.8 61.2 all-reduce.6
  459.4 47.5 all-gather.1
where the time goes:
time: 634 us; the launch traced here: 622 us
  waiting for transfers between devices  242 us (38%)
  matrix products  168 us (26%)
  local copies, waits for them, and re-layouts  81.4 us (13%)
  other arithmetic  76.7 us (12%)
  blocking collectives  23.3 us (4%)
  starting transfers between devices  16.3 us (3%)
  between operations  14.4 us (2%)
    all_to_all x1, waiting for transfers between devices, body(): lax.all_to_all(packed, 'sky', split_axis=1, concat_axis=1, tiled=True)  136 us
    dot_general x8, matrix products, add_sender(): jnp.einsum('ctk,tks->cts', portion, within, precision=lax.Precision.HIGHEST)  79.5 us
    psum x1, waiting for transfers between devices, body(): summed = lax.psum(normals, 'tm')  61.1 us
    another operation x1, local copies, waits for them, and re-layouts, body(): jnp.stack(products + [scaled[first] * arrived[0] for first in range(5)])  49.6 us
    mul x2, other arithmetic, body(): scaled[first] * arrived[0]  43.1 us
    all_gather x1, waiting for transfers between devices, body(): everything = lax.all_gather(source_update, 'sky', axis=1, tiled=True)  40.7 us
    dot_general x8, matrix products, fill(): jnp.einsum('cts,tks->ctk', row_values, within, precision=lax.Precision.HI...  38 us
    dot_general x8, matrix products, add_sender(): jnp.einsum('cts,tp->cps', spread, pixel_hits, precision=lax.Precision.HIG...  25.8 us
  transfers between devices with their start and end apart: 6, of which 5 were waited for; matrix products, arithmetic and copies ran while one was open for 16% of the time, Pallas kernels for 0%

commit v1 on v0

v1 whole, which is shorter than its diff:
```python
import functools

import jax
import jax.numpy as jnp
from jax import lax
from jax.experimental import pallas as pl
from jax.experimental.pallas import tpu as pltpu
from jax.sharding import PartitionSpec as P

PIX_DEV = 128
SRC_PIX = 128
KNOTS_DEV = 512


SOURCE_PAIRS = tuple(((first, second) for first in range(5) for second in range(first, 5)))
KNOT_PAIRS = tuple(((first, second) for first in range(4) for second in range(first, 4)))


def passed_along(value, axes, steps):
    count = 1
    for axis in axes:
        count *= lax.axis_size(axis)
    first, last = (max(0, -steps), min(count, count - steps))
    return lax.ppermute(value, axes, [(source, source + steps) for source in range(first, last)])


def damped_solve(normal, target, order, pairs):
    entries = {}
    for number, couple in enumerate(pairs):
        entries[couple] = normal[number]
    factor = {}
    for column in range(order):
        pivot_value = entries[column, column] + 1.0
        for earlier in range(column):
            pivot_value = pivot_value - factor[column, earlier] * factor[column, earlier]
        pivot_value = jnp.sqrt(pivot_value)
        factor[column, column] = pivot_value
        for below in range(column + 1, order):
            current = entries[column, below]
            for earlier in range(column):
                current = current - factor[below, earlier] * factor[column, earlier]
            factor[below, column] = current / pivot_value
    forward = []
    for column in range(order):
        current = target[column]
        for earlier in range(column):
            current = current - factor[column, earlier] * forward[earlier]
        forward.append(current / factor[column, column])
    answer = [None] * order
    for column in reversed(range(order)):
        current = forward[column]
        for later in range(column + 1, order):
            current = current - factor[later, column] * answer[later]
        answer[column] = current / factor[column, column]
    return jnp.stack(answer)


ROWS = 20
PAD = 24


def sums_kernel(pixel_ref, slot_ref, resid, weight, parts, index, out, acc, stage):
    tiles = resid.shape[0]
    chunks, _, run, _ = out.shape
    pixels = chunks * run

    def clear(step, carry):
        acc[pl.ds(pl.multiple_of(step * 192, 192), 192), :] = jnp.zeros((192, SRC_PIX), jnp.float32)
        return carry

    lax.fori_loop(0, pixels * PAD // 192, clear, 0)
    stage[...] = jnp.zeros_like(stage)
    sources = lax.broadcasted_iota(jnp.int32, (SRC_PIX, SRC_PIX), 0)

    def group(step, carry):
        base = pl.multiple_of(step * 8, 8)
        here = pl.ds(base, 8)
        fields = [parts[c, here, :] for c in range(5)]
        scaled = [weight[here, :] * field for field in fields]
        baseline = resid[here, :]
        row = 0
        for first, second in SOURCE_PAIRS:
            stage[pl.ds(row, 8, stride=PAD), :] = scaled[first] * fields[second]
            row += 1
        for first in range(5):
            stage[pl.ds(row, 8, stride=PAD), :] = scaled[first] * baseline
            row += 1
        ids = index[here, :]
        for j in range(8):
            seat = slot_ref[pixel_ref[base + j]]
            values = stage[j * PAD : (j + 1) * PAD, :]
            high = values.astype(jnp.bfloat16)
            low = (values - high.astype(jnp.float32)).astype(jnp.bfloat16)
            hits = jnp.where(sources == ids[j : j + 1, :], 1.0, 0.0).astype(jnp.bfloat16)
            both = lax.dot_general(
                jnp.concatenate([high, low], axis=0),
                hits,
                (((1,), (1,)), ((), ())),
                preferred_element_type=jnp.float32,
            )
            spot = pl.ds(pl.multiple_of(seat * PAD, 8), PAD)
            acc[spot, :] += both[:PAD] + both[PAD:]
        return carry

    lax.fori_loop(0, tiles // 8, group, 0)

    def unload(chunk, carry):
        for row in range(ROWS):
            for part in range(run // 8):
                start = (chunk * run + part * 8) * PAD + row
                out[chunk, row, part * 8 : part * 8 + 8, :] = acc[pl.ds(start, 8, stride=PAD), :]
        return carry

    lax.fori_loop(0, chunks, unload, 0)


def local_sums(tile_pixel, pixel_slot, residual, obs_weight, source_partials, source_index, chunks):
    pixels = pixel_slot.shape[0]
    return pl.pallas_call(
        sums_kernel,
        name="local_sums",
        out_shape=jax.ShapeDtypeStruct((chunks, ROWS, pixels // chunks, SRC_PIX), jnp.float32),
        in_specs=[pl.BlockSpec(memory_space=pltpu.SMEM)] * 2
        + [pl.BlockSpec(memory_space=pltpu.VMEM)] * 4,
        out_specs=pl.BlockSpec(memory_space=pltpu.VMEM),
        scratch_shapes=[
            pltpu.VMEM((pixels * PAD, SRC_PIX), jnp.float32),
            pltpu.VMEM((8 * PAD, SRC_PIX), jnp.float32),
        ],
        compiler_params=pltpu.CompilerParams(vmem_limit_bytes=60 * 1024 * 1024),
    )(tile_pixel, pixel_slot, residual, obs_weight, source_partials, source_index)


def settle_kernel(run, pixel_ref, slot_ref, resid, parts, index, table, out, rows):
    tiles = resid.shape[0]

    def group(step, carry):
        base = pl.multiple_of(step * 8, 8)
        here = pl.ds(base, 8)
        for j in range(8):
            seat = slot_ref[pixel_ref[base + j]]
            start = (seat // run) * (5 * run) + seat % run
            for c in range(5):
                rows[c, pl.ds(base + j, 1), :] = table[pl.ds(start + c * run, 1), :]
        ids = index[here, :]
        total = None
        for c in range(5):
            picked = jnp.take_along_axis(rows[c, here, :], ids, axis=1)
            addend = parts[c, here, :] * picked
            total = addend if total is None else total + addend
        out[here, :] = resid[here, :] - total
        return carry

    lax.fori_loop(0, tiles // 8, group, 0)


def settle(tile_pixel, pixel_slot, residual, source_partials, source_index, table, run):
    tiles = residual.shape[0]
    return pl.pallas_call(
        functools.partial(settle_kernel, run),
        name="settle",
        out_shape=jax.ShapeDtypeStruct(residual.shape, jnp.float32),
        in_specs=[pl.BlockSpec(memory_space=pltpu.SMEM)] * 2
        + [pl.BlockSpec(memory_space=pltpu.VMEM)] * 4,
        out_specs=pl.BlockSpec(memory_space=pltpu.VMEM),
        scratch_shapes=[pltpu.VMEM((5, tiles, SRC_PIX), jnp.float32)],
        compiler_params=pltpu.CompilerParams(vmem_limit_bytes=48 * 1024 * 1024),
    )(tile_pixel, pixel_slot, residual, source_partials, source_index, table)


def tile_rows(weights, partials, baseline, couples):
    rows = []
    for segment in range(4):
        portion = partials[4 * segment : 4 * segment + 4]
        for first, second in couples:
            other = baseline if second is None else portion[second]
            rows.append(jnp.sum(weights * portion[first] * other, axis=-1))
    return jnp.stack(rows)


def on_knots(rows, knot_hits, span):
    placed = jnp.dot(rows, knot_hits, precision=lax.Precision.HIGHEST)
    count = rows.shape[0] // 4
    total = jnp.zeros((count, span + 3), jnp.float32)
    for segment in range(4):
        part = placed[count * segment : count * (segment + 1)]
        total = total + jnp.pad(part, ((0, 0), (segment, 3 - segment)))
    return total


def body(
    residual,
    obs_weight,
    source_partials,
    attitude_partials,
    source_index,
    tile_pixel,
    tile_knot,
    pixel_slot,
):
    owners = lax.axis_size("sky")
    times = lax.axis_size("tm")
    chunks = owners * times
    run = PIX_DEV // times
    span = KNOTS_DEV // owners
    block = lax.axis_index("tm") * owners + lax.axis_index("sky")

    sums = local_sums(
        tile_pixel, pixel_slot, residual, obs_weight, source_partials, source_index, chunks
    )
    summed = reduce_chunks(sums)

    knot_start = tile_knot - block * span
    knot_hits = (knot_start[:, None] == jnp.arange(span, dtype=jnp.int32)[None, :]).astype(
        jnp.float32
    )
    square_rows = tile_rows(obs_weight, attitude_partials, None, KNOT_PAIRS)
    squares = on_knots(square_rows, knot_hits, span)

    update = damped_solve(summed[:15], summed[15:], 5, SOURCE_PAIRS)
    table = lax.all_gather(update, ("sky", "tm"), axis=0, tiled=False)
    settled = settle(
        tile_pixel,
        pixel_slot,
        residual,
        source_partials,
        source_index,
        table.reshape(chunks * 5 * run, SRC_PIX),
        run,
    )
    mine = lax.dynamic_slice_in_dim(table, lax.axis_index("sky") * times, times, 0)
    source_update = mine.transpose(1, 0, 2, 3).reshape(5, PIX_DEV * SRC_PIX)

    target_rows = tile_rows(
        obs_weight, attitude_partials, settled, [(first, None) for first in range(4)]
    )
    targets = on_knots(target_rows, knot_hits, span)
    accumulated = jnp.concatenate([squares, targets], axis=0)
    axes = ("tm", "sky")
    arriving = passed_along(accumulated[:, span:], axes, 1)
    whole = accumulated[:, :span] + jnp.pad(arriving, ((0, 0), (0, span - 3)))
    own_update = damped_solve(whole[:10], whole[10:], 4, KNOT_PAIRS)
    following = passed_along(own_update[:, :3], axes, -1)
    extended = jnp.concatenate([own_update, following], axis=1)
    attitude_update = lax.all_gather(own_update, "sky", axis=1, tiled=True)
    windows = jnp.concatenate([extended[:, seg : seg + span] for seg in range(4)], axis=0)
    values = jnp.dot(windows, knot_hits.T, precision=lax.Precision.HIGHEST)
    total = None
    for number in range(16):
        addend = attitude_partials[number] * values[number][:, None]
        total = addend if total is None else total + addend
    return (settled - total, source_update, attitude_update)


def reduce_chunks(sums):
    part = lax.psum_scatter(sums, ("sky", "tm"), scatter_dimension=0, tiled=True)
    return part[0]


def solution(mesh):
    in_specs = (
        P(("tm", "sky"), None),
        P(("tm", "sky"), None),
        P(None, ("tm", "sky"), None),
        P(None, ("tm", "sky"), None),
        P(("tm", "sky"), None),
        P(("tm", "sky")),
        P(("tm", "sky")),
        P(),
    )
    out_specs = (P(("tm", "sky"), None), P(None, "sky"), P(None, "tm"))
    return jax.shard_map(body, mesh=mesh, in_specs=in_specs, out_specs=out_specs, check_vma=False)
```

time: 634 us -> 377 us (0.59); the launches traced: 622 us -> 377 us
  matrix products: 168 us -> 0.88 us
  local copies, waits for them, and re-layouts: 81.4 us -> 5.56 us
  other arithmetic: 76.7 us -> 15.9 us
  waiting for transfers between devices: 242 us -> 282 us
  Pallas kernels: 0 us -> 36.2 us
  blocking collectives: 23.3 us -> 13.3 us
  starting transfers between devices: 16.3 us -> 8.79 us
    reduce_scatter x0 -> x1, waiting for transfers between devices: none -> 226 us  [reduce_chunks(): lax.psum_scatter(sums, ('sky', 'tm'), scatter_dimension=0, tiled=True)]
    dot_general x44 -> x3, matrix products: 168 us -> 0.88 us  [the longest x2 0.57 us: on_knots(): placed = jnp.dot(rows, knot_hits, precision=lax.Precision.HIGHEST)]
    all_to_all x2 -> x0, waiting for transfers between devices: 136 us -> none  [the longest x1 136 us: body(): lax.all_to_all(packed, 'sky', split_axis=1, concat_axis=1, tiled=True)]
    psum x1 -> x0, waiting for transfers between devices: 61.1 us -> none  [body(): summed = lax.psum(normals, 'tm')]
    another operation x5 -> x2, local copies, waits for them, and re-layouts: 49.9 us -> 0.27 us  [tile_rows(): return jnp.stack(rows)]
    mul x4 -> x0, other arithmetic: 43.2 us -> none  [the longest x2 43.1 us: body(): scaled[first] * arrived[0]]
    pallas_call x0 -> x2, Pallas kernels: none -> 36.2 us  [the longest x1 27.7 us: local_sums(): pl.pallas_call(sums_kernel, name='local_sums', out_shape=jax.ShapeDtypeSt...]
    psum x1 -> x0, blocking collectives: 23.3 us -> none  [body(): whole = lax.psum(own_rows, 'sky')]
  transfers between devices with their start and end apart: 6 -> 4, of which waited for: 5 -> 2; matrix products, arithmetic and copies ran while one was open for 16% -> 2% of each run, Pallas kernels for 0% -> 0%
where the time goes in v1:
time: 377 us
  waiting for transfers between devices  282 us (75%)
  Pallas kernels  36.2 us (10%)
  other arithmetic  15.9 us (4%)
  between operations  14.3 us (4%)
  blocking collectives  13.3 us (4%)
  starting transfers between devices  8.79 us (2%)
  local copies, waits for them, and re-layouts  5.56 us (1%)
    reduce_scatter x1, waiting for transfers between devices, reduce_chunks(): lax.psum_scatter(sums, ('sky', 'tm'), scatter_dimension=0, tiled=True)  226 us
    all_gather x1, waiting for transfers between devices, body(): table = lax.all_gather(update, ('sky', 'tm'), axis=0, tiled=False)  55.9 us
    pallas_call x1, Pallas kernels, local_sums(): pl.pallas_call(sums_kernel, name='local_sums', out_shape=jax.ShapeDtypeSt...  27.7 us
    all_gather x1, blocking collectives, body(): attitude_update = lax.all_gather(own_update, 'sky', axis=1, tiled=True)  13.3 us
    ppermute x2, starting transfers between devices, passed_along(): lax.ppermute(value, axes, [(source, source + steps) for source in range(f...  8.71 us
    pallas_call x1, Pallas kernels, settle(): pl.pallas_call(functools.partial(settle_kernel, run), name='settle', out_...  8.46 us
    reduce_sum x4, other arithmetic, tile_rows(): rows.append(jnp.sum(weights * portion[first] * other, axis=-1))  8.07 us
  transfers between devices with their start and end apart: 4, of which 2 were waited for; matrix products, arithmetic and copies ran while one was open for 2% of the time, Pallas kernels for 0%

profile of v1, /device:TPU:5, one launch (start us, length us, event | category | flops | bytes accessed | tf_op | source)
XLA Modules:
  0.0 376.6 jit_solution(2351883874546658891)
XLA Ops:
  7.2 27.7 %local_sums.1 = f32[32,20,32,128]{3,2,1,0:T(8,128)} custom-call(s32[512]{0:T(512)} %pixel_ref.3, s32[1024]{0:T(1024)} %slot_ref.3, f32[512,128]{1,0:T(8,128)} %resid.3, f32[512,128]{1,0:T(8,128)} %weight.1, f32[5,512,128]{2,1,0:T(8,128)} %parts.3, s32[512,128]{1,0:T(8,128)} %index.3), custom_call_target="tpu_custom_call" | custom-call | tf_op jit(solution)/shard_map/local_sums/pallas_call | solution.py:119
  35.0 225.7 %reduce-scatter.2.cloned.1.call-done = f32[1,20,32,128]{3,2,1,0:T(8,128)} async-done(((f32[32,20,32,128]{3,2,1,0:T(8,128)}), f32[1,20,32,128]{3,2,1,0:T(8,128)}) %reduce-scatter.2.cloned.1.call-update) | async-done | bytes 327696 | tf_op jit(solution)/shard_map/reduce_scatter | solution.py:256
  260.7 0.9 fusion.98
  261.7 1.0 fusion.105
  262.6 0.9 divide_dynamic-update-slice_fusion
  263.6 0.6 copy-done.10
  264.3 3.1 fusion.8
  267.4 2.8 fusion.1
  270.2 55.9 %all-gather.4.cloned.1.call-done = f32[160,32,128]{2,1,0:T(8,128)} async-done(((f32[5,32,128]{2,1,0:T(8,128)}), f32[160,32,128]{2,1,0:T(8,128)}) %all-gather.4.cloned.1.call-update) | async-done | bytes 2621456 | tf_op jit(solution)/shard_map/all_gather | solution.py:221
  326.1 1.7 copy-done.1
  327.9 8.5 %settle.1 = f32[512,128]{1,0:T(8,128)S(1)} custom-call(s32[512]{0:T(512)S(1)} %copy-done.5, s32[1024]{0:T(1024)S(1)} %copy-done.4, f32[512,128]{1,0:T(8,128)S(1)} %copy-done.2, f32[5,512,128]{2,1,0:T(8,128)S(1)} %copy-done, s32[512,128]{1,0:T(8,128)S(1)} %copy-done.3, f32[5120,128]{1,0:T(8,128)S(1)} %bitcast.591), custom_call_target="tpu_custom_call" | custom-call | tf_op jit(solution)/shard_map/settle/pallas_call | solution.py:159
  336.3 1.0 fusion.3
  337.4 1.2 fusion
  338.5 0.2 stack.230
  338.7 0.3 fusion.58
  339.1 0.3 fusion.57
  339.7 2.6 collective-permute-start
  342.3 1.0 dynamic-slice_bitcast_fusion
  343.3 1.0 copy.18
  344.5 6.1 %collective-permute-start.1 = (f32[4,3]{1,0:T(4,128)S(1)}, f32[4,3]{1,0:T(4,128)S(1)}, u32[]{:S(2)}, u32[]{:S(2)}) collective-permute-start(f32[4,3]{1,0:T(4,128)S(1)} %bitcast.667), channel_id=1, source_target_pairs={{1,0},{2,1},{3,2},{4,3},{5,4},{6,5},{7,6},{8,7},{9,8},{10,9},{11,1... | collective-permute-start | bytes 152 | tf_op jit(solution)/shard_map/ppermute | solution.py:24
  350.6 13.3 %all-gather.1 = f32[8,64,4]{1,2,0:T(4,128)S(1)} all-gather(f32[1,64,4]{1,2,0:T(4,128)S(1)} %get-tuple-element.153), channel_id=1, replica_groups=mesh['tm'=4,'sky'=8] {'sky'}, dimensions={0}, use_global_device_ids=true | all-gather | bytes 9216 | tf_op jit(solution)/shard_map/all_gather | solution.py:245
  363.9 0.7 reshape.877
  364.8 0.3 fusion.56
  365.1 4.6 %fusion.5 = f32[512,128]{1,0:T(8,128)} fusion(f32[512,128]{1,0:T(8,128)S(1)} %settle.1, f32[16,512,128]{2,1,0:T(8,128)} %param.11, f32[512]{0:T(512)S(1)} %bitcast.638, f32[512]{0:T(512)S(1)} %bitcast.639, f32[512]{0:T(512)S(1)} %bitcast.640, f32[512]{0:T(512)S(1)} %bitcast.641, f32[512]{0:T(512)S(1)} %bitcast.642, f32[512]{0:T(512)S(1)} %bitcast.643, ...), kind=kLoop, calls=%fused_computation.13 | loop fusion | flops 2097152 | bytes 4751360 | tf_op jit(solution)/shard_map/sub | solution.py:252
  (50 shorter events, 0.9 us)
Async XLA Ops:
  7.2 253.5 %reduce-scatter.2.cloned.1.call-start = ((), (), s32[]{:S(2)}) async-start(), calls=%async_computation.1 | async-start | bytes 10813440 | tf_op jit(solution)/shard_map/reduce_scatter | solution.py:256
  34.9 229.3 %copy-start.11 = (s32[512]{0:T(512)S(1)}, s32[512]{0:T(512)}, u32[]{:S(2)}) copy-start(s32[512]{0:T(512)} %param.14) | copy-start | bytes 6148
  34.9 229.3 %copy-start.7 = (f32[512,128]{1,0:T(8,128)S(1)}, f32[512,128]{1,0:T(8,128)}, u32[]{:S(2)}) copy-start(f32[512,128]{1,0:T(8,128)} %weight.1) | copy-start | bytes 786436
  35.0 291.1 %all-gather.4.cloned.1.call-start = ((), (), s32[]{:S(2)}) async-start(), calls=%async_computation.2 | async-start | bytes 2703360 | tf_op jit(solution)/shard_map/all_gather | solution.py:221
  261.6 64.5 %copy-start = (f32[5,512,128]{2,1,0:T(8,128)S(1)}, f32[5,512,128]{2,1,0:T(8,128)}, u32[]{:S(2)}) copy-start(f32[5,512,128]{2,1,0:T(8,128)} %parts.3) | copy-start | bytes 3932164
  261.6 64.5 %copy-start.2 = (f32[512,128]{1,0:T(8,128)S(1)}, f32[512,128]{1,0:T(8,128)}, u32[]{:S(2)}) copy-start(f32[512,128]{1,0:T(8,128)} %resid.3) | copy-start | bytes 786436
  261.6 64.5 %copy-start.3 = (s32[512,128]{1,0:T(8,128)S(1)}, s32[512,128]{1,0:T(8,128)}, u32[]{:S(2)}) copy-start(s32[512,128]{1,0:T(8,128)} %index.3) | copy-start | bytes 786436
  261.6 64.5 %copy-start.4 = (s32[1024]{0:T(1024)S(1)}, s32[1024]{0:T(1024)}, u32[]{:S(2)}) copy-start(s32[1024]{0:T(1024)} %slot_ref.3) | copy-start | bytes 12292
  261.6 64.5 %copy-start.5 = (s32[512]{0:T(512)S(1)}, s32[512]{0:T(512)}, u32[]{:S(2)}) copy-start(s32[512]{0:T(512)} %pixel_ref.3) | copy-start | bytes 6148
  263.6 0.6 copy-start.10
  326.1 1.7 copy-start.1
  327.9 8.5 %copy-start.6 = (f32[16,512,128]{2,1,0:T(8,128)S(1)}, f32[16,512,128]{2,1,0:T(8,128)}, u32[]{:S(2)}) copy-start(f32[16,512,128]{2,1,0:T(8,128)} %param.11) | copy-start | bytes 12582916
  327.9 9.5 %copy-start.8 = (f32[512,128]{1,0:T(8,128)S(1)}, f32[512,128]{1,0:T(8,128)}, u32[]{:S(2)}) copy-start(f32[512,128]{1,0:T(8,128)} %get-tuple-element.105) | copy-start | bytes 786436
  327.9 9.5 %copy-start.9 = (f32[512,128]{1,0:T(8,128)S(1)}, f32[512,128]{1,0:T(8,128)}, u32[]{:S(2)}) copy-start(f32[512,128]{1,0:T(8,128)} %get-tuple-element.106) | copy-start | bytes 786436
  339.7 4.7 %collective-permute-start = (f32[14,3]{1,0:T(8,128)S(1)}, f32[14,3]{1,0:T(8,128)S(1)}, u32[]{:S(2)}, u32[]{:S(2)}) collective-permute-start(f32[14,3]{1,0:T(8,128)S(1)} %pad_maximum_fusion), channel_id=1, source_target_pairs={{0,1},{1,2},{2,3},{3,4},{4,5},{5,6},{6,7},{7,8},{8,9},{9,10},{10,1... | collective-permute-start | bytes 512 | tf_op jit(solution)/shard_map/ppermute | solution.py:24
  344.5 20.1 %collective-permute-start.1 = (f32[4,3]{1,0:T(4,128)S(1)}, f32[4,3]{1,0:T(4,128)S(1)}, u32[]{:S(2)}, u32[]{:S(2)}) collective-permute-start(f32[4,3]{1,0:T(4,128)S(1)} %bitcast.667), channel_id=1, source_target_pairs={{1,0},{2,1},{3,2},{4,3},{5,4},{6,5},{7,6},{8,7},{9,8},{10,9},{11,1... | collective-permute-start | bytes 152 | tf_op jit(solution)/shard_map/ppermute | solution.py:24
Sparse Core Ops, SparseCore 0:
  35.1 225.5 reduce-scatter.1
  264.4 61.6 all-gather.3

commit v2 on v1

--- a/solution.py
+++ b/solution.py
@@ -208,13 +208,13 @@
     sums = local_sums(
         tile_pixel, pixel_slot, residual, obs_weight, source_partials, source_index, chunks
     )
-    summed = reduce_chunks(sums)
+    summed, late_weight = lax.optimization_barrier((reduce_chunks(sums), obs_weight))
 
     knot_start = tile_knot - block * span
     knot_hits = (knot_start[:, None] == jnp.arange(span, dtype=jnp.int32)[None, :]).astype(
         jnp.float32
     )
-    square_rows = tile_rows(obs_weight, attitude_partials, None, KNOT_PAIRS)
+    square_rows = tile_rows(late_weight, attitude_partials, None, KNOT_PAIRS)
     squares = on_knots(square_rows, knot_hits, span)
 
     update = damped_solve(summed[:15], summed[15:], 5, SOURCE_PAIRS)
@@ -252,9 +252,117 @@
     return (settled - total, source_update, attitude_update)
 
 
+def add_rows(count, target, *sources):
+    def one(row, carry):
+        total = sources[0][row]
+        for source in sources[1:]:
+            total = total + source[row]
+        target[row] = total
+        return carry
+
+    lax.fori_loop(0, count, one, 0)
+
+
+def reduce_kernel(times, lines, sums, out, got0, got1, part, got2, *sems):
+    send0, recv0, send1, recv1, send2, recv2 = sems
+    mesh_ids = pl.DeviceIdType.MESH
+    time, sky = lax.axis_index("tm"), lax.axis_index("sky")
+    line, core = sky // 2, sky % 2
+    time_peers = [lax.rem(time + step, times) for step in range(1, times)]
+    line_peers = [lax.rem(line + step, lines) for step in range(1, lines)]
+    partner = (time, sky + 1 - 2 * core)
+
+    barrier = pltpu.get_barrier_semaphore()
+    peers = [partner] + [(peer, sky) for peer in time_peers]
+    peers += [(time, peer * 2 + core) for peer in line_peers]
+    for peer in peers:
+        pl.semaphore_signal(barrier, inc=1, device_id=peer, device_id_type=mesh_ids)
+    pl.semaphore_wait(barrier, len(peers))
+
+    pieces = line_peers + [line]
+    first = []
+    for step, piece in enumerate(pieces):
+        copy = pltpu.make_async_remote_copy(
+            src_ref=sums.at[piece, 1 - core],
+            dst_ref=got0.at[step],
+            send_sem=send0.at[step],
+            recv_sem=recv0.at[step],
+            device_id=partner,
+            device_id_type=mesh_ids,
+        )
+        copy.start()
+        first.append(copy)
+    second = []
+    for step, piece in enumerate(pieces):
+        first[step].wait_recv()
+        for slot in range(times):
+            target = got0.at[step, slot]
+            add_rows(ROWS, target, target, sums.at[piece, core, slot])
+        copies = []
+        for number, peer in enumerate(time_peers):
+            copy = pltpu.make_async_remote_copy(
+                src_ref=got0.at[step, peer],
+                dst_ref=got1.at[step, number],
+                send_sem=send1.at[step, number],
+                recv_sem=recv1.at[step, number],
+                device_id=(peer, sky),
+                device_id_type=mesh_ids,
+            )
+            copy.start()
+            copies.append(copy)
+        second.append(copies)
+    third = []
+    for step, piece in enumerate(pieces):
+        for copy in second[step]:
+            copy.wait_recv()
+        arrived = [got1.at[step, number] for number in range(times - 1)]
+        add_rows(ROWS, part.at[step], got0.at[step, time], *arrived)
+        if step < lines - 1:
+            copy = pltpu.make_async_remote_copy(
+                src_ref=part.at[step],
+                dst_ref=got2.at[step],
+                send_sem=send2.at[step],
+                recv_sem=recv2.at[step],
+                device_id=(time, piece * 2 + core),
+                device_id_type=mesh_ids,
+            )
+            copy.start()
+            third.append(copy)
+    for copy in third:
+        copy.wait_recv()
+    arrived = [got2.at[step] for step in range(lines - 1)]
+    add_rows(ROWS, out, part.at[lines - 1], *arrived)
+    for copy in first + [copy for copies in second for copy in copies] + third:
+        copy.wait_send()
+
+
 def reduce_chunks(sums):
-    part = lax.psum_scatter(sums, ("sky", "tm"), scatter_dimension=0, tiled=True)
-    return part[0]
+    times, owners = lax.axis_size("tm"), lax.axis_size("sky")
+    lines = owners // 2
+    unit = sums.shape[1:]
+    dma = pltpu.SemaphoreType.DMA
+    return pl.pallas_call(
+        functools.partial(reduce_kernel, times, lines),
+        name="reduce_chunks",
+        out_shape=jax.ShapeDtypeStruct(unit, jnp.float32),
+        in_specs=[pl.BlockSpec(memory_space=pltpu.VMEM)],
+        out_specs=pl.BlockSpec(memory_space=pltpu.VMEM),
+        scratch_shapes=[
+            pltpu.VMEM((lines, times) + unit, jnp.float32),
+            pltpu.VMEM((lines, times - 1) + unit, jnp.float32),
+            pltpu.VMEM((lines,) + unit, jnp.float32),
+            pltpu.VMEM((lines - 1,) + unit, jnp.float32),
+            dma((lines,)),
+            dma((lines,)),
+            dma((lines, times - 1)),
+            dma((lines, times - 1)),
+            dma((lines - 1,)),
+            dma((lines - 1,)),
+        ],
+        compiler_params=pltpu.CompilerParams(
+            collective_id=0, has_side_effects=True, vmem_limit_bytes=62 * 1024 * 1024
+        ),
+    )(sums.reshape((lines, 2, times) + unit))
 
 
 def solution(mesh):

time: 377 us -> 216 us (0.57)
  waiting for transfers between devices: 282 us -> 50.9 us
  Pallas kernels: 36.2 us -> 107 us
    reduce_scatter x1 -> x0, waiting for transfers between devices: 226 us -> none  [reduce_chunks(): lax.psum_scatter(sums, ('sky', 'tm'), scatter_dimension=0, tiled=True)]
    pallas_call x0 -> x1, Pallas kernels: none -> 71 us  [reduce_chunks(): pl.pallas_call(functools.partial(reduce_kernel, times, lines), name='redu...]
    all_gather x1, waiting for transfers between devices: 55.9 us -> 50.8 us  [body(): table = lax.all_gather(update, ('sky', 'tm'), axis=0, tiled=False)]
    reduce_sum x4 -> x3, other arithmetic: 8.07 us -> 3.24 us  [tile_rows(): rows.append(jnp.sum(weights * portion[first] * other, axis=-1))]
  transfers between devices with their start and end apart: 4 -> 3, of which waited for: 2 -> 1; matrix products, arithmetic and copies ran while one was open for 2% -> 4% of each run, Pallas kernels for 0% -> 0%
where the time goes in v2:
time: 216 us; the launch traced here: 215 us
  Pallas kernels  107 us (50%)
  waiting for transfers between devices  50.9 us (24%)
  other arithmetic  14.4 us (7%)
  between operations  14.3 us (7%)
  blocking collectives  13.3 us (6%)
  starting transfers between devices  8.75 us (4%)
  local copies, waits for them, and re-layouts  5.6 us (3%)
    pallas_call x1, Pallas kernels, reduce_chunks(): pl.pallas_call(functools.partial(reduce_kernel, times, lines), name='redu...  71 us
    all_gather x1, waiting for transfers between devices, body(): table = lax.all_gather(update, ('sky', 'tm'), axis=0, tiled=False)  50.8 us
    pallas_call x1, Pallas kernels, local_sums(): pl.pallas_call(sums_kernel, name='local_sums', out_shape=jax.ShapeDtypeSt...  27.7 us
    all_gather x1, blocking collectives, body(): attitude_update = lax.all_gather(own_update, 'sky', axis=1, tiled=True)  13.3 us
    ppermute x2, starting transfers between devices, passed_along(): lax.ppermute(value, axes, [(source, source + steps) for source in range(f...  8.71 us
    pallas_call x1, Pallas kernels, settle(): pl.pallas_call(functools.partial(settle_kernel, run), name='settle', out_...  8.46 us
    sub x1, other arithmetic, body(): return (settled - total, source_update, attitude_update)  4.58 us
  transfers between devices with their start and end apart: 3, of which 1 were waited for; matrix products, arithmetic and copies ran while one was open for 4% of the time, Pallas kernels for 0%

profile of v2, /device:TPU:5, one launch (start us, length us, event | category | flops | bytes accessed | tf_op | source)
XLA Modules:
  0.0 215.3 jit_solution(5428899915254529789)
XLA Ops:
  7.2 27.7 %local_sums.1 = f32[32,20,32,128]{3,2,1,0:T(8,128)} custom-call(s32[512]{0:T(512)} %pixel_ref.3, s32[1024]{0:T(1024)} %slot_ref.3, f32[512,128]{1,0:T(8,128)} %resid.3, f32[512,128]{1,0:T(8,128)} %weight.1, f32[5,512,128]{2,1,0:T(8,128)} %parts.3, s32[512,128]{1,0:T(8,128)} %index.3), custom_call_target="tpu_custom_call" | custom-call | tf_op jit(solution)/shard_map/local_sums/pallas_call | solution.py:119
  34.9 71.0 %reduce_chunks.1 = f32[20,32,128]{2,1,0:T(8,128)} custom-call(f32[4,2,4,20,32,128]{5,4,3,2,1,0:T(8,128)} %bitcast.433), custom_call_target="tpu_custom_call" | custom-call | tf_op jit(solution)/shard_map/reduce_chunks/pallas_call | solution.py:344
  105.9 0.9 subtract_divide_fusion.7
  106.9 0.9 subtract_divide_fusion.9
  107.8 0.9 divide_dynamic-update-slice_fusion
  108.8 0.6 copy-done.9
  109.4 3.4 %bitcast_multiply_fusion.59 = (f32[512,128]{1,0:T(8,128)S(1)}, f32[512,128]{1,0:T(8,128)S(1)}, f32[512,128]{1,0:T(8,128)S(1)}, f32[512]{0:T(512)S(1)}, f32[512]{...) fusion(f32[512,128]{1,0:T(8,128)S(1)} %copy-done.8, ...), kind=kLoop, calls=%fused_computation.129 | loop fusion | flops 2810880 | bytes 5533696 | tf_op jit(solution)/shard_map/mul | solution.py:177
  112.9 0.9 fusion.4
  113.8 1.1 fusion.3
  114.9 0.2 stack.230
  115.1 0.3 fusion.90
  115.5 50.8 %all-gather.4.cloned.1.call-done = f32[160,32,128]{2,1,0:T(8,128)} async-done(((f32[5,32,128]{2,1,0:T(8,128)}), f32[160,32,128]{2,1,0:T(8,128)}) %all-gather.4.cloned.1.call-update) | async-done | bytes 2621456 | tf_op jit(solution)/shard_map/all_gather | solution.py:221
  166.4 1.7 copy-done.1
  168.1 8.5 %settle.1 = f32[512,128]{1,0:T(8,128)S(1)} custom-call(s32[512]{0:T(512)S(1)} %copy-done.5, s32[1024]{0:T(1024)S(1)} %copy-done.4, f32[512,128]{1,0:T(8,128)S(1)} %copy-done.2, f32[5,512,128]{2,1,0:T(8,128)S(1)} %copy-done, s32[512,128]{1,0:T(8,128)S(1)} %copy-done.3, f32[5120,128]{1,0:T(8,128)S(1)} %bitcast.432), custom_call_target="tpu_custom_call" | custom-call | tf_op jit(solution)/shard_map/settle/pallas_call | solution.py:159
  176.6 1.3 fusion.10
  177.9 0.3 fusion.89
  178.4 2.6 %collective-permute-start = (f32[14,3]{1,0:T(8,128)S(1)}, f32[14,3]{1,0:T(8,128)S(1)}, u32[]{:S(2)}, u32[]{:S(2)}) collective-permute-start(f32[14,3]{1,0:T(8,128)S(1)} %pad_maximum_fusion), channel_id=1, source_target_pairs={{0,1},{1,2},{2,3},{3,4},{4,5},{5,6},{6,7},{7,8},{8,9},{9,10},{10,1... | collective-permute-start | bytes 512 | tf_op jit(solution)/shard_map/ppermute | solution.py:24
  181.0 1.0 dynamic-slice_bitcast_fusion
  182.0 1.0 copy.18
  183.2 6.1 %collective-permute-start.1 = (f32[4,3]{1,0:T(4,128)S(1)}, f32[4,3]{1,0:T(4,128)S(1)}, u32[]{:S(2)}, u32[]{:S(2)}) collective-permute-start(f32[4,3]{1,0:T(4,128)S(1)} %bitcast.509), channel_id=1, source_target_pairs={{1,0},{2,1},{3,2},{4,3},{5,4},{6,5},{7,6},{8,7},{9,8},{10,9},{11,1... | collective-permute-start | bytes 152 | tf_op jit(solution)/shard_map/ppermute | solution.py:24
  189.3 13.3 %all-gather.1 = f32[8,64,4]{1,2,0:T(4,128)S(1)} all-gather(f32[1,64,4]{1,2,0:T(4,128)S(1)} %get-tuple-element.150), channel_id=1, replica_groups=mesh['tm'=4,'sky'=8] {'sky'}, dimensions={0}, use_global_device_ids=true | all-gather | bytes 9216 | tf_op jit(solution)/shard_map/all_gather | solution.py:245
  202.6 0.7 reshape.38
  203.5 0.3 fusion.88
  203.8 4.6 %fusion.8 = f32[512,128]{1,0:T(8,128)} fusion(f32[512,128]{1,0:T(8,128)S(1)} %settle.1, f32[16,512,128]{2,1,0:T(8,128)} %param.11, f32[512]{0:T(512)S(1)} %bitcast.477, f32[512]{0:T(512)S(1)} %bitcast.478, f32[512]{0:T(512)S(1)} %bitcast.479, f32[512]{0:T(512)S(1)} %bitcast.480, f32[512]{0:T(512)S(1)} %bitcast.481, f32[512]{0:T(512)S(1)} %bitcast.482, ...), kind=kLoop, calls=%fused_computation.19 | loop fusion | flops 2097152 | bytes 4751360 | tf_op jit(solution)/shard_map/sub | solution.py:252
  (46 shorter events, 0.9 us)
Async XLA Ops:
  7.2 159.2 %all-gather.4.cloned.1.call-start = ((), (), s32[]{:S(2)}) async-start(), calls=%async_computation | async-start | bytes 2703360 | tf_op jit(solution)/shard_map/all_gather | solution.py:221
  34.9 74.5 %copy-start.8 = (f32[512,128]{1,0:T(8,128)S(1)}, f32[512,128]{1,0:T(8,128)}, u32[]{:S(2)}) copy-start(f32[512,128]{1,0:T(8,128)} %weight.1) | copy-start | bytes 786436
  108.7 0.6 copy-start.9
  109.4 3.4 %copy-start.6 = (f32[16,512,128]{2,1,0:T(8,128)S(1)}, f32[16,512,128]{2,1,0:T(8,128)}, u32[]{:S(2)}) copy-start(f32[16,512,128]{2,1,0:T(8,128)} %param.11) | copy-start | bytes 12582916
  112.8 2.3 %copy-start.10 = (s32[512]{0:T(512)S(1)}, s32[512]{0:T(512)}, u32[]{:S(2)}) copy-start(s32[512]{0:T(512)} %param.14) | copy-start | bytes 6148
  112.9 53.5 %copy-start = (f32[5,512,128]{2,1,0:T(8,128)S(1)}, f32[5,512,128]{2,1,0:T(8,128)}, u32[]{:S(2)}) copy-start(f32[5,512,128]{2,1,0:T(8,128)} %parts.3) | copy-start | bytes 3932164
  112.9 53.5 %copy-start.2 = (f32[512,128]{1,0:T(8,128)S(1)}, f32[512,128]{1,0:T(8,128)}, u32[]{:S(2)}) copy-start(f32[512,128]{1,0:T(8,128)} %resid.3) | copy-start | bytes 786436
  112.9 53.5 %copy-start.3 = (s32[512,128]{1,0:T(8,128)S(1)}, s32[512,128]{1,0:T(8,128)}, u32[]{:S(2)}) copy-start(s32[512,128]{1,0:T(8,128)} %index.3) | copy-start | bytes 786436
  112.9 53.5 %copy-start.4 = (s32[1024]{0:T(1024)S(1)}, s32[1024]{0:T(1024)}, u32[]{:S(2)}) copy-start(s32[1024]{0:T(1024)} %slot_ref.3) | copy-start | bytes 12292
  112.9 53.5 %copy-start.5 = (s32[512]{0:T(512)S(1)}, s32[512]{0:T(512)}, u32[]{:S(2)}) copy-start(s32[512]{0:T(512)} %pixel_ref.3) | copy-start | bytes 6148
  166.4 1.7 copy-start.1
  168.1 8.5 %copy-start.7 = (f32[16,512,128]{2,1,0:T(8,128)S(1)}, f32[16,512,128]{2,1,0:T(8,128)}, u32[]{:S(2)}) copy-start(f32[16,512,128]{2,1,0:T(8,128)} %param.11) | copy-start | bytes 12582916
  178.4 4.7 %collective-permute-start = (f32[14,3]{1,0:T(8,128)S(1)}, f32[14,3]{1,0:T(8,128)S(1)}, u32[]{:S(2)}, u32[]{:S(2)}) collective-permute-start(f32[14,3]{1,0:T(8,128)S(1)} %pad_maximum_fusion), channel_id=1, source_target_pairs={{0,1},{1,2},{2,3},{3,4},{4,5},{5,6},{6,7},{7,8},{8,9},{9,10},{10,1... | collective-permute-start | bytes 512 | tf_op jit(solution)/shard_map/ppermute | solution.py:24
  183.2 20.1 %collective-permute-start.1 = (f32[4,3]{1,0:T(4,128)S(1)}, f32[4,3]{1,0:T(4,128)S(1)}, u32[]{:S(2)}, u32[]{:S(2)}) collective-permute-start(f32[4,3]{1,0:T(4,128)S(1)} %bitcast.509), channel_id=1, source_target_pairs={{1,0},{2,1},{3,2},{4,3},{5,4},{6,5},{7,6},{8,7},{9,8},{10,9},{11,1... | collective-permute-start | bytes 152 | tf_op jit(solution)/shard_map/ppermute | solution.py:24
Sparse Core Ops, SparseCore 0:
  109.5 56.7 all-gather.3

commit v3 on v2

--- a/solution.py
+++ b/solution.py
@@ -218,7 +218,7 @@
     squares = on_knots(square_rows, knot_hits, span)
 
     update = damped_solve(summed[:15], summed[15:], 5, SOURCE_PAIRS)
-    table = lax.all_gather(update, ("sky", "tm"), axis=0, tiled=False)
+    table = gather_chunks(update)
     settled = settle(
         tile_pixel,
         pixel_slot,
@@ -365,6 +365,88 @@
     )(sums.reshape((lines, 2, times) + unit))
 
 
+def gather_kernel(times, lines, update, table, send0, recv0, send1, recv1, send2, recv2):
+    mesh_ids = pl.DeviceIdType.MESH
+    time, sky = lax.axis_index("tm"), lax.axis_index("sky")
+    line, core = sky // 2, sky % 2
+    time_peers = [lax.rem(time + step, times) for step in range(1, times)]
+    line_peers = [lax.rem(line + step, lines) for step in range(1, lines)]
+    partner = (time, sky + 1 - 2 * core)
+
+    barrier = pltpu.get_barrier_semaphore()
+    peers = [partner] + [(peer, sky) for peer in time_peers]
+    peers += [(time, peer * 2 + core) for peer in line_peers]
+    for peer in peers:
+        pl.semaphore_signal(barrier, inc=1, device_id=peer, device_id_type=mesh_ids)
+    pl.semaphore_wait(barrier, len(peers))
+
+    def send(source, target, send_sem, recv_sem, peer):
+        copy = pltpu.make_async_remote_copy(
+            src_ref=source,
+            dst_ref=target,
+            send_sem=send_sem,
+            recv_sem=recv_sem,
+            device_id=peer,
+            device_id_type=mesh_ids,
+        )
+        copy.start()
+        return copy
+
+    own = table.at[sky * times + time]
+    first = []
+    for number, peer in enumerate(line_peers):
+        spot = (time, peer * 2 + core)
+        first.append(send(update, own, send0.at[number], recv0.at[number], spot))
+    own[...] = update[...]
+    sources = [line] + [lax.rem(line + lines - step, lines) for step in range(1, lines)]
+    second = []
+    for step, source in enumerate(sources):
+        place = table.at[(source * 2 + core) * times + time]
+        if step > 0:
+            first[step - 1].wait_recv()
+        held = place if step > 0 else update
+        second.append(
+            [
+                send(held, place, send1.at[step, number], recv1.at[step, number], (peer, sky))
+                for number, peer in enumerate(time_peers)
+            ]
+        )
+    third = []
+    for step, source in enumerate(sources):
+        for copy in second[step]:
+            copy.wait_recv()
+        place = table.at[pl.ds((source * 2 + core) * times, times)]
+        third.append(send(place, place, send2.at[step], recv2.at[step], partner))
+    for copy in third:
+        copy.wait_recv()
+    for copy in first + [copy for copies in second for copy in copies] + third:
+        copy.wait_send()
+
+
+def gather_chunks(update):
+    times, owners = lax.axis_size("tm"), lax.axis_size("sky")
+    lines = owners // 2
+    dma = pltpu.SemaphoreType.DMA
+    return pl.pallas_call(
+        functools.partial(gather_kernel, times, lines),
+        name="gather_chunks",
+        out_shape=jax.ShapeDtypeStruct((owners * times,) + update.shape, jnp.float32),
+        in_specs=[pl.BlockSpec(memory_space=pltpu.VMEM)],
+        out_specs=pl.BlockSpec(memory_space=pltpu.VMEM),
+        scratch_shapes=[
+            dma((lines - 1,)),
+            dma((lines - 1,)),
+            dma((lines, times - 1)),
+            dma((lines, times - 1)),
+            dma((lines,)),
+            dma((lines,)),
+        ],
+        compiler_params=pltpu.CompilerParams(
+            collective_id=1, has_side_effects=True, vmem_limit_bytes=16 * 1024 * 1024
+        ),
+    )(update)
+
+
 def solution(mesh):
     in_specs = (
         P(("tm", "sky"), None),

time: 216 us -> 168 us (0.78)
  waiting for transfers between devices: 50.9 us -> 0.01 us
  Pallas kernels: 107 us -> 127 us
  between operations: 14.3 us -> 0.95 us
    all_gather x1 -> x0, waiting for transfers between devices: 50.8 us -> none  [body(): table = lax.all_gather(update, ('sky', 'tm'), axis=0, tiled=False)]
    pallas_call x0 -> x1, Pallas kernels: none -> 19.6 us  [gather_chunks(): pl.pallas_call(functools.partial(gather_kernel, times, lines), name='gath...]
  transfers between devices with their start and end apart: 3 -> 2, of which waited for: 1 -> 0; matrix products, arithmetic and copies ran while one was open for 4% -> 1% of each run, Pallas kernels for 0% -> 0%
where the time goes in v3:
time: 168 us
  Pallas kernels  127 us (76%)
  other arithmetic  13.6 us (8%)
  blocking collectives  12.6 us (8%)
  starting transfers between devices  9.49 us (6%)
  local copies, waits for them, and re-layouts  3.64 us (2%)
    pallas_call x1, Pallas kernels, reduce_chunks(): pl.pallas_call(functools.partial(reduce_kernel, times, lines), name='redu...  71 us
    pallas_call x1, Pallas kernels, local_sums(): pl.pallas_call(sums_kernel, name='local_sums', out_shape=jax.ShapeDtypeSt...  27.7 us
    pallas_call x1, Pallas kernels, gather_chunks(): pl.pallas_call(functools.partial(gather_kernel, times, lines), name='gath...  19.6 us
    all_gather x1, blocking collectives, body(): attitude_update = lax.all_gather(own_update, 'sky', axis=1, tiled=True)  12.6 us
    ppermute x2, starting transfers between devices, passed_along(): lax.ppermute(value, axes, [(source, source + steps) for source in range(f...  9.49 us
    pallas_call x1, Pallas kernels, settle(): pl.pallas_call(functools.partial(settle_kernel, run), name='settle', out_...  8.46 us
    reduce_sum x3, other arithmetic, tile_rows(): rows.append(jnp.sum(weights * portion[first] * other, axis=-1))  5.03 us
    sub x1, other arithmetic, body(): return (settled - total, source_update, attitude_update)  4.58 us
  transfers between devices with their start and end apart: 2, of which 0 were waited for; matrix products, arithmetic and copies ran while one was open for 1% of the time, Pallas kernels for 0%

profile of v3, /device:TPU:5, one launch (start us, length us, event | category | flops | bytes accessed | tf_op | source)
XLA Modules:
  0.0 168.0 jit_solution(16441820691305906666)
XLA Ops:
  0.6 27.7 %local_sums.1 = f32[32,20,32,128]{3,2,1,0:T(8,128)} custom-call(s32[512]{0:T(512)} %pixel_ref.3, s32[1024]{0:T(1024)} %slot_ref.3, f32[512,128]{1,0:T(8,128)} %resid.3, f32[512,128]{1,0:T(8,128)} %weight.1, f32[5,512,128]{2,1,0:T(8,128)} %parts.3, s32[512,128]{1,0:T(8,128)} %index.3), custom_call_target="tpu_custom_call" | custom-call | tf_op jit(solution)/shard_map/local_sums/pallas_call | solution.py:119
  28.4 71.0 %reduce_chunks.1 = f32[20,32,128]{2,1,0:T(8,128)} custom-call(f32[4,2,4,20,32,128]{5,4,3,2,1,0:T(8,128)} %bitcast.431), custom_call_target="tpu_custom_call" | custom-call | tf_op jit(solution)/shard_map/reduce_chunks/pallas_call | solution.py:344
  99.4 3.3 %bitcast_multiply_fusion.59 = (f32[512,128]{1,0:T(8,128)S(1)}, f32[512,128]{1,0:T(8,128)S(1)}, f32[512,128]{1,0:T(8,128)S(1)}, f32[512]{0:T(512)S(1)}, f32[512]{...) fusion(f32[512,128]{1,0:T(8,128)S(1)} %copy-done.7, ...), kind=kLoop, calls=%fused_computation.129 | loop fusion | flops 2810880 | bytes 5533696 | tf_op jit(solution)/shard_map/mul | solution.py:177
  102.7 0.1 copy-done.5
  102.8 1.1 fusion.3
  104.0 2.8 %fusion.4 = (f32[512]{0:T(512)S(1)}, f32[512]{0:T(512)S(1)}, f32[512]{0:T(512)S(1)}, f32[512]{0:T(512)S(1)}, f32[512]{0:T(512)S(1)}, /*index=5*/f32[512]{0:T(512...) fusion(f32[512,128]{1,0:T(8,128)S(1)} %get-tuple-element.102, ...), kind=kLoop, calls=%fused_computation.15 | loop fusion | flops 1566720 | bytes 3956736 | tf_op jit(solution)/shard_map/reduce_sum | solution.py:177
  106.7 0.2 stack.230
  106.9 0.3 fusion.90
  107.4 0.1 divide_dynamic-update-slice_fusion
  107.5 19.6 %gather_chunks.1 = f32[32,5,32,128]{3,2,1,0:T(8,128)S(1)} custom-call(f32[5,32,128]{2,1,0:T(8,128)S(1)} %constant_dynamic-update-slice_fusion.update), custom_call_target="tpu_custom_call" | custom-call | tf_op jit(solution)/shard_map/gather_chunks/pallas_call | solution.py:430
  127.2 1.3 copy-done
  128.5 8.5 %settle.1 = f32[512,128]{1,0:T(8,128)S(1)} custom-call(s32[512]{0:T(512)S(1)} %copy-done.4, s32[1024]{0:T(1024)S(1)} %copy-done.3, f32[512,128]{1,0:T(8,128)S(1)} %copy-done.1, f32[5,512,128]{2,1,0:T(8,128)S(1)} %copy-done, s32[512,128]{1,0:T(8,128)S(1)} %copy-done.2, f32[5120,128]{1,0:T(8,128)S(1)} %bitcast.430), custom_call_target="tpu_custom_call" | custom-call | tf_op jit(solution)/shard_map/settle/pallas_call | solution.py:159
  137.0 1.2 fusion.10
  138.2 0.1 stack.247
  138.2 0.3 fusion.89
  138.5 0.1 pad_add_fusion
  138.7 0.1 pad_maximum_fusion
  138.8 2.2 %collective-permute-start = (f32[14,3]{1,0:T(8,128)S(1)}, f32[14,3]{1,0:T(8,128)S(1)}, u32[]{:S(2)}, u32[]{:S(2)}) collective-permute-start(f32[14,3]{1,0:T(8,128)S(1)} %pad_maximum_fusion), channel_id=1, source_target_pairs={{0,1},{1,2},{2,3},{3,4},{4,5},{5,6},{6,7},{7,8},{8,9},{9,10},{10,1... | collective-permute-start | bytes 512 | tf_op jit(solution)/shard_map/ppermute | solution.py:24
  141.1 1.0 copy.17
  142.2 7.3 %collective-permute-start.1 = (f32[4,3]{1,0:T(4,128)S(1)}, f32[4,3]{1,0:T(4,128)S(1)}, u32[]{:S(2)}, u32[]{:S(2)}) collective-permute-start(f32[4,3]{1,0:T(4,128)S(1)} %bitcast.507), channel_id=1, source_target_pairs={{1,0},{2,1},{3,2},{4,3},{5,4},{6,5},{7,6},{8,7},{9,8},{10,9},{11,1... | collective-permute-start | bytes 152 | tf_op jit(solution)/shard_map/ppermute | solution.py:24
  149.5 12.6 %all-gather = f32[8,64,4]{1,2,0:T(4,128)S(1)} all-gather(f32[1,64,4]{1,2,0:T(4,128)S(1)} %get-tuple-element.150), channel_id=1, replica_groups=mesh['tm'=4,'sky'=8] {'sky'}, dimensions={0}, use_global_device_ids=true | all-gather | bytes 9216 | tf_op jit(solution)/shard_map/all_gather | solution.py:245
  162.1 0.7 reshape.36
  163.0 0.3 fusion.88
  163.4 4.6 %fusion.8 = f32[512,128]{1,0:T(8,128)} fusion(f32[512,128]{1,0:T(8,128)S(1)} %settle.1, f32[16,512,128]{2,1,0:T(8,128)} %param.11, f32[512]{0:T(512)S(1)} %bitcast.475, f32[512]{0:T(512)S(1)} %bitcast.476, f32[512]{0:T(512)S(1)} %bitcast.477, f32[512]{0:T(512)S(1)} %bitcast.478, f32[512]{0:T(512)S(1)} %bitcast.479, f32[512]{0:T(512)S(1)} %bitcast.480, ...), kind=kLoop, calls=%fused_computation.19 | loop fusion | flops 2097152 | bytes 4751360 | tf_op jit(solution)/shard_map/sub | solution.py:252
  (44 shorter events, 0.7 us)
Async XLA Ops:
  28.4 71.0 %copy-start.7 = (f32[512,128]{1,0:T(8,128)S(1)}, f32[512,128]{1,0:T(8,128)}, u32[]{:S(2)}) copy-start(f32[512,128]{1,0:T(8,128)} %weight.1) | copy-start | bytes 786436
  99.4 3.4 %copy-start.5 = (f32[16,512,128]{2,1,0:T(8,128)S(1)}, f32[16,512,128]{2,1,0:T(8,128)}, u32[]{:S(2)}) copy-start(f32[16,512,128]{2,1,0:T(8,128)} %param.11) | copy-start | bytes 12582916
  99.4 4.6 %copy-start.10 = (s32[512]{0:T(512)S(1)}, s32[512]{0:T(512)}, u32[]{:S(2)}) copy-start(s32[512]{0:T(512)} %param.14) | copy-start | bytes 6148
  102.8 4.4 %copy-start.9 = (f32[20,32,128]{2,1,0:T(8,128)S(1)}, f32[20,32,128]{2,1,0:T(8,128)}, u32[]{:S(2)}) copy-start(f32[20,32,128]{2,1,0:T(8,128)} %reduce_chunks.1) | copy-start | bytes 983044
  103.9 23.2 %copy-start.1 = (f32[512,128]{1,0:T(8,128)S(1)}, f32[512,128]{1,0:T(8,128)}, u32[]{:S(2)}) copy-start(f32[512,128]{1,0:T(8,128)} %resid.3) | copy-start | bytes 786436
  103.9 23.2 %copy-start.2 = (s32[512,128]{1,0:T(8,128)S(1)}, s32[512,128]{1,0:T(8,128)}, u32[]{:S(2)}) copy-start(s32[512,128]{1,0:T(8,128)} %index.3) | copy-start | bytes 786436
  103.9 23.2 %copy-start.3 = (s32[1024]{0:T(1024)S(1)}, s32[1024]{0:T(1024)}, u32[]{:S(2)}) copy-start(s32[1024]{0:T(1024)} %slot_ref.3) | copy-start | bytes 12292
  103.9 23.2 %copy-start.4 = (s32[512]{0:T(512)S(1)}, s32[512]{0:T(512)}, u32[]{:S(2)}) copy-start(s32[512]{0:T(512)} %pixel_ref.3) | copy-start | bytes 6148
  107.3 29.7 %copy-start.8 = (f32[512,128]{1,0:T(8,128)S(1)}, f32[512,128]{1,0:T(8,128)}, u32[]{:S(2)}) copy-start(f32[512,128]{1,0:T(8,128)} %weight.1) | copy-start | bytes 786436
  127.2 1.3 copy-start
  128.5 8.5 %copy-start.6 = (f32[16,512,128]{2,1,0:T(8,128)S(1)}, f32[16,512,128]{2,1,0:T(8,128)}, u32[]{:S(2)}) copy-start(f32[16,512,128]{2,1,0:T(8,128)} %param.11) | copy-start | bytes 12582916
  138.8 3.3 %collective-permute-start = (f32[14,3]{1,0:T(8,128)S(1)}, f32[14,3]{1,0:T(8,128)S(1)}, u32[]{:S(2)}, u32[]{:S(2)}) collective-permute-start(f32[14,3]{1,0:T(8,128)S(1)} %pad_maximum_fusion), channel_id=1, source_target_pairs={{0,1},{1,2},{2,3},{3,4},{4,5},{5,6},{6,7},{7,8},{8,9},{9,10},{10,1... | collective-permute-start | bytes 512 | tf_op jit(solution)/shard_map/ppermute | solution.py:24
  142.2 20.6 %collective-permute-start.1 = (f32[4,3]{1,0:T(4,128)S(1)}, f32[4,3]{1,0:T(4,128)S(1)}, u32[]{:S(2)}, u32[]{:S(2)}) collective-permute-start(f32[4,3]{1,0:T(4,128)S(1)} %bitcast.507), channel_id=1, source_target_pairs={{1,0},{2,1},{3,2},{4,3},{5,4},{6,5},{7,6},{8,7},{9,8},{10,9},{11,1... | collective-permute-start | bytes 152 | tf_op jit(solution)/shard_map/ppermute | solution.py:24
